TPU v7x, 256 devices: a 4x2x16 block of a 4x16x16 slice. The times are simulated.
256 devices in a mesh: groups: 2 (over y), expert: 32 (over z, core), tensor: 4 (over x).
Axes of the slice: x: 4, y: 2, z: 16, core: 2. Of those that a mesh axis runs over, the one named last changes fastest.
The devices are a block of a 4x16x16 slice.
Arguments:
- tokens: bfloat16 [8192, 6144], P(('groups', 'expert', 'tensor')), parts along dimension 0, may hold values from -6 to 6
- expert_ids: int32 [8192, 2], P(('groups', 'expert', 'tensor')), parts along dimension 0, may hold values from 0 to 31, all different within a row; in each aligned block of 32 rows (0 to 31, 32 to 63, ...) at most 4 rows name the same one
- gate_scores: float32 [8192, 2], P(('groups', 'expert', 'tensor')), parts along dimension 0, may hold values from 0.1 to 1
- norm_gain: float32 [6144], replicated, may hold values from 0.1 to 1.9
- w_gate: bfloat16 [32, 6144, 1024], P('expert', None, 'tensor'), may hold values from -0.078125 to 0.078125
- w_up: bfloat16 [32, 6144, 1024], P('expert', None, 'tensor'), may hold values from -0.078125 to 0.078125
- w_down: bfloat16 [32, 1024, 6144], P('expert', 'tensor'), may hold values from -0.1875 to 0.1875
Outputs:
- mixed: bfloat16 [8192, 6144], P(('groups', 'expert', 'tensor')), parts along dimension 0
There are 2 independent parts, one for each index of `groups`. A program takes and returns all parts, laid end to end along the dimension named above; an argument that names none is the same for every part. Nothing has to cross between parts.
Inputs may be any that keep to these rules, and one draw needn't show every extreme that they name: `expert_ids`: each token names 2 different experts. Within the 32 tokens of one device, no expert is named more than 4 times, a bound that some block reaches.
All inputs are finite; a program needn't handle non-finite values.
Results may differ from a plain program's by a relative error of at most 0.011.
Values may be sent and summed in bfloat16 or wider, within the bound.
A program may use at most 64 MiB of HBM per device.

v0:
```python
import jax
import jax.numpy as jnp
from jax import lax
from jax.sharding import PartitionSpec as P


def on_device(tokens, expert_ids, gate_scores, norm_gain, w_gate, w_up, w_down):
    rows = tokens.shape[0]
    width = tokens.shape[1]
    picks = expert_ids.shape[1]
    experts = lax.axis_size("expert")
    capacity = 4 * rows // experts
    values = tokens.astype(jnp.float32)
    scale = lax.rsqrt(jnp.mean(values * values, axis=-1, keepdims=True) + 1e-05)
    normed = (values * scale * norm_gain).astype(jnp.bfloat16)
    flat_ids = expert_ids.reshape(-1)
    onehot = (flat_ids[:, None] == jnp.arange(experts, dtype=jnp.int32)[None, :]).astype(jnp.int32)
    earlier = jnp.cumsum(onehot, axis=0) - onehot
    slot = jnp.sum(earlier * onehot, axis=1)
    target = flat_ids * capacity + slot
    placing = jnp.arange(experts * capacity, dtype=jnp.int32)[:, None] == target[None, :]
    placing = placing.reshape(experts * capacity, rows, picks)
    place_tok = jnp.sum(placing.astype(jnp.float32), axis=2).astype(jnp.bfloat16)
    weighting = jnp.sum(placing.astype(jnp.float32) * gate_scores[None, :, :], axis=2)
    outgoing = jnp.dot(place_tok, normed, preferred_element_type=jnp.float32).astype(jnp.bfloat16)
    outgoing = outgoing.reshape(experts, capacity, width)
    arrived = lax.all_to_all(outgoing, "expert", split_axis=0, concat_axis=0, tiled=True)
    arrived = arrived.reshape(-1, width)
    piece = lax.all_gather(arrived, "tensor", axis=0, tiled=True)
    gate = jnp.dot(piece, w_gate[0], preferred_element_type=jnp.float32)
    up = jnp.dot(piece, w_up[0], preferred_element_type=jnp.float32)
    hidden = (jax.nn.silu(gate) * up).astype(jnp.bfloat16)
    parts = jnp.dot(hidden, w_down[0], preferred_element_type=jnp.float32)
    summed = lax.psum_scatter(parts.astype(jnp.bfloat16), "tensor", scatter_dimension=0, tiled=True)
    summed = summed.reshape(experts, capacity, width)
    results = lax.all_to_all(summed, "expert", split_axis=0, concat_axis=0, tiled=True)
    results = results.reshape(experts * capacity, width)
    mixed = jnp.dot(weighting.T, results.astype(jnp.float32), preferred_element_type=jnp.float32)
    return mixed.astype(jnp.bfloat16)


def solution(mesh):
    return jax.shard_map(
        on_device,
        mesh=mesh,
        in_specs=(
            P(("groups", "expert", "tensor"), None),
            P(("groups", "expert", "tensor"), None),
            P(("groups", "expert", "tensor"), None),
            P(),
            P("expert", None, "tensor"),
            P("expert", None, "tensor"),
            P("expert", "tensor", None),
        ),
        out_specs=P(("groups", "expert", "tensor"), None),
        check_vma=False,
    )
```

profile of v0, /device:TPU:33, one launch (start us, length us, event | category | flops | bytes accessed | tf_op | source)
XLA Modules:
  0.0 381.0 jit_solution(17998000077517687781)
XLA Ops:
  6.6 1.3 fusion.11
  7.9 0.8 copy.20
  8.7 0.1 eq.30
  8.8 0.1 fusion.17
  8.8 0.1 reduce_window_sum.11
  8.9 0.2 select_reduce_fusion.1
  9.1 0.1 reduce_sum.39
  9.2 0.1 copy.21
  9.3 0.7 multiply_add_fusion
  10.0 0.8 convert_reduce_fusion
  10.8 2.8 convolution_convert_fusion.1
  13.6 3.8 reshape.41
  17.4 103.9 %all_to_all.10 = bf16[32,4,6144]{2,1,0:T(4,128)(2,1)} all-to-all(bf16[32,4,6144]{2,1,0:T(4,128)(2,1)} %reshape.41), channel_id=1, replica_groups=mesh['groups'=2,'expert'=32,'tensor'=4] {'expert'}, dimensions={0} | all-to-all | bytes 3145728 | tf_op jit(solution)/shard_map/all_to_all | solution.py:27
  121.2 3.6 reshape.42
  125.0 63.8 %all-gather.2.cloned.1.call-done = bf16[512,6144]{1,0:T(8,128)(2,1)} async-done(((bf16[128,6144]{1,0:T(8,128)(2,1)}), bf16[512,6144]{1,0:T(8,128)(2,1)}) %all-gather.2.cloned.1.call-update) | async-done | bytes 6291472 | tf_op jit(solution)/shard_map/all_gather | solution.py:29
  188.8 5.6 %fusion.3 = f32[512,256]{1,0:T(8,128)S(1)} fusion(bf16[512,6144]{1,0:T(8,128)(2,1)} %all-gather.2.cloned.1.call-done, bf16[1,6144,256]{2,1,0:T(8,128)(2,1)} %param.11), kind=kOutput, calls=%fused_computation.6 | convolution fusion | flops 1610612736 | bytes 9961472 | tf_op jit(solution)/shard_map/dot_general | solution.py:30
  194.5 0.8 copy-done.2
  195.3 1.8 fusion.8
  197.1 4.5 %convolution_convert_fusion = bf16[512,6144]{1,0:T(8,128)(2,1)} fusion(bf16[512,256]{1,0:T(8,128)(2,1)S(1)} %fusion.8, bf16[1,256,6144]{2,1,0:T(8,128)(2,1)S(1)} %copy-done), kind=kOutput, calls=%fused_computation | convolution fusion | flops 1613758464 | bytes 9699328 | tf_op jit(solution)/shard_map/dot_general | solution.py:33
  201.6 71.0 %reduce-scatter.2.cloned.1.call-done = bf16[128,6144]{1,0:T(8,128)(2,1)} async-done(((bf16[512,6144]{1,0:T(8,128)(2,1)}), bf16[128,6144]{1,0:T(8,128)(2,1)}) %reduce-scatter.2.cloned.1.call-update) | async-done | bytes 1572880 | tf_op jit(solution)/shard_map/reduce_scatter | solution.py:34
  272.6 3.8 reshape.43
  276.4 91.6 %all_to_all.11 = bf16[32,4,6144]{2,1,0:T(4,128)(2,1)} all-to-all(bf16[32,4,6144]{2,1,0:T(4,128)(2,1)} %reshape.43), channel_id=1, replica_groups=mesh['groups'=2,'expert'=32,'tensor'=4] {'expert'}, dimensions={0} | all-to-all | bytes 3145728 | tf_op jit(solution)/shard_map/all_to_all | solution.py:36
  368.0 3.7 reshape.44
  371.6 2.5 fusion.19
  (10 shorter events, 0.2 us)
Async XLA Ops:
  6.5 190.5 %copy-start = (bf16[1,256,6144]{2,1,0:T(8,128)(2,1)S(1)}, bf16[1,256,6144]{2,1,0:T(8,128)(2,1)}, u32[]{:S(2)}) copy-start(bf16[1,256,6144]{2,1,0:T(8,128)(2,1)} %param.13) | copy-start | bytes 9437188
  6.6 182.3 %all-gather.2.cloned.1.call-start = ((), (), s32[]{:S(2)}) async-start(), calls=%async_computation.3 | async-start | bytes 7864320 | tf_op jit(solution)/shard_map/all_gather | solution.py:29
  124.9 147.7 %reduce-scatter.2.cloned.1.call-start = ((), (), s32[]{:S(2)}) async-start(), calls=%async_computation.4 | async-start | bytes 7864320 | tf_op jit(solution)/shard_map/reduce_scatter | solution.py:34
  188.8 5.7 %copy-start.1 = (bf16[512,6144]{1,0:T(8,128)(2,1)S(1)}, bf16[512,6144]{1,0:T(8,128)(2,1)}, u32[]{:S(2)}) copy-start(bf16[512,6144]{1,0:T(8,128)(2,1)} %all-gather.2.cloned.1.call-done) | copy-start | bytes 18874372
  188.8 6.4 %copy-start.2 = (bf16[1,6144,256]{2,1,0:T(8,128)(2,1)S(1)}, bf16[1,6144,256]{2,1,0:T(8,128)(2,1)}, u32[]{:S(2)}) copy-start(bf16[1,6144,256]{2,1,0:T(8,128)(2,1)} %param.12) | copy-start | bytes 9437188
Sparse Core Ops, SparseCore 0:
  125.0 63.7 all-gather.1
  201.7 70.8 reduce-scatter.1
where the time goes:
time: 382 us; the launch traced here: 381 us
  blocking collectives  195 us (51%)
  waiting for transfers between devices  135 us (35%)
  matrix products  17.2 us (5%)
  local copies, waits for them, and re-layouts  16.7 us (4%)
  between operations  13.5 us (4%)
    all_to_all x1, blocking collectives, on_device(): lax.all_to_all(outgoing, 'expert', split_axis=0, concat_axis=0, tiled=True)  104 us
    all_to_all x1, blocking collectives, on_device(): lax.all_to_all(summed, 'expert', split_axis=0, concat_axis=0, tiled=True)  91.6 us
    reduce_scatter x1, waiting for transfers between devices, on_device(): lax.psum_scatter(parts.astype(jnp.bfloat16), 'tensor', scatter_dimension=...  71 us
    all_gather x1, waiting for transfers between devices, on_device(): piece = lax.all_gather(arrived, 'tensor', axis=0, tiled=True)  63.8 us
  transfers between devices with their start and end apart: 2, of which 2 were waited for; matrix products, arithmetic and copies ran while one was open for 0% of the time, Pallas kernels for 0%

commit v1 on v0

--- a/solution.py
+++ b/solution.py
@@ -2,6 +2,11 @@
 import jax.numpy as jnp
 from jax import lax
 from jax.sharding import PartitionSpec as P
+
+
+def tiled_gather(value, axis, dim):
+    copies = jnp.concatenate([value] * lax.axis_size(axis), axis=dim)
+    return lax.all_to_all(copies, axis, dim, dim, tiled=True)
 
 
 def on_device(tokens, expert_ids, gate_scores, norm_gain, w_gate, w_up, w_down):
@@ -26,7 +31,7 @@
     outgoing = outgoing.reshape(experts, capacity, width)
     arrived = lax.all_to_all(outgoing, "expert", split_axis=0, concat_axis=0, tiled=True)
     arrived = arrived.reshape(-1, width)
-    piece = lax.all_gather(arrived, "tensor", axis=0, tiled=True)
+    piece = tiled_gather(arrived, "tensor", 0)
     gate = jnp.dot(piece, w_gate[0], preferred_element_type=jnp.float32)
     up = jnp.dot(piece, w_up[0], preferred_element_type=jnp.float32)
     hidden = (jax.nn.silu(gate) * up).astype(jnp.bfloat16)

time: 382 us -> 382 us (level)
  blocking collectives: 195 us -> 270 us
  waiting for transfers between devices: 135 us -> 61.4 us
  other arithmetic: 3.14 us -> 7.12 us
  matrix products: 17.2 us -> 13.3 us
    all_to_all x0 -> x1, blocking collectives: none -> 74.6 us  [tiled_gather(): return lax.all_to_all(copies, axis, dim, dim, tiled=True)]
    all_gather x1 -> x0, waiting for transfers between devices: 63.8 us -> none  [on_device(): piece = lax.all_gather(arrived, 'tensor', axis=0, tiled=True)]
    reduce_scatter x1, waiting for transfers between devices: 71 us -> 61.3 us  [on_device(): lax.psum_scatter(parts.astype(jnp.bfloat16), 'tensor', scatter_dimension=...]
    concatenate x0 -> x1, other arithmetic: none -> 3.98 us  [tiled_gather(): copies = jnp.concatenate([value] * lax.axis_size(axis), axis=dim)]
    dot_general x1, matrix products: 5.64 us -> 1.79 us  [on_device(): gate = jnp.dot(piece, w_gate[0], preferred_element_type=jnp.float32)]
  transfers between devices with their start and end apart: 2 -> 1, of which waited for: 2 -> 1; matrix products, arithmetic and copies ran while one was open for 0% -> 0% of each run, Pallas kernels for 0% -> 0%
where the time goes in v1:
time: 382 us; the launch traced here: 381 us
  blocking collectives  270 us (71%)
  waiting for transfers between devices  61.4 us (16%)
  local copies, waits for them, and re-layouts  16.1 us (4%)
  between operations  13.5 us (4%)
  matrix products  13.3 us (3%)
  other arithmetic  7.12 us (2%)
    all_to_all x1, blocking collectives, on_device(): lax.all_to_all(outgoing, 'expert', split_axis=0, concat_axis=0, tiled=True)  104 us
    all_to_all x1, blocking collectives, on_device(): lax.all_to_all(summed, 'expert', split_axis=0, concat_axis=0, tiled=True)  91.6 us
    all_to_all x1, blocking collectives, tiled_gather(): return lax.all_to_all(copies, axis, dim, dim, tiled=True)  74.6 us
    reduce_scatter x1, waiting for transfers between devices, on_device(): lax.psum_scatter(parts.astype(jnp.bfloat16), 'tensor', scatter_dimension=...  61.3 us
  transfers between devices with their start and end apart: 1, of which 1 were waited for; matrix products, arithmetic and copies ran while one was open for 0% of the time, Pallas kernels for 0%

profile of v1, /device:TPU:33, one launch (start us, length us, event | category | flops | bytes accessed | tf_op | source)
XLA Modules:
  0.0 381.5 jit_solution(9887857108300863155)
XLA Ops:
  6.6 1.3 fusion.11
  7.9 0.8 copy.20
  8.7 0.1 eq.30
  8.8 0.1 reduce_window_sum.11
  8.9 0.2 select_reduce_fusion.1
  9.1 0.1 reduce_sum.39
  9.2 0.1 copy.21
  9.3 0.7 multiply_add_fusion
  10.0 0.8 convert_reduce_fusion
  10.8 2.8 convolution_convert_fusion.1
  13.6 3.8 reshape.43
  17.4 103.9 %all_to_all.22 = bf16[32,4,6144]{2,1,0:T(4,128)(2,1)} all-to-all(bf16[32,4,6144]{2,1,0:T(4,128)(2,1)} %reshape.43), channel_id=1, replica_groups=mesh['groups'=2,'expert'=32,'tensor'=4] {'expert'}, dimensions={0} | all-to-all | bytes 3145728 | tf_op jit(solution)/shard_map/all_to_all | solution.py:32
  121.2 3.7 reshape.44
  124.9 4.0 %pad_maximum_fusion = bf16[512,6144]{1,0:T(8,128)(2,1)S(1)} fusion(bf16[128,6144]{1,0:T(8,128)(2,1)} %reshape.44), kind=kLoop, calls=%fused_computation.3 | loop fusion | flops 25165824 | bytes 7864320 | tf_op jit(solution)/shard_map/concatenate | solution.py:8
  128.9 74.6 %all_to_all.23 = bf16[4,128,6144]{2,1,0:T(8,128)(2,1)S(1)} all-to-all(bf16[4,128,6144]{2,1,0:T(8,128)(2,1)S(1)} %bitcast.21), channel_id=1, replica_groups=mesh['groups'=2,'expert'=32,'tensor'=4] {'tensor'}, dimensions={0} | all-to-all | bytes 12582912 | tf_op jit(solution)/shard_map/all_to_all | solution.py:9
  203.5 1.8 fusion.3
  205.3 0.1 copy-done.2
  205.4 1.8 fusion.8
  207.2 4.5 %convolution_convert_fusion = bf16[512,6144]{1,0:T(8,128)(2,1)} fusion(bf16[512,256]{1,0:T(8,128)(2,1)S(1)} %fusion.8, bf16[1,256,6144]{2,1,0:T(8,128)(2,1)S(1)} %copy-done), kind=kOutput, calls=%fused_computation | convolution fusion | flops 1613758464 | bytes 9699328 | tf_op jit(solution)/shard_map/dot_general | solution.py:38
  211.8 61.3 %reduce-scatter.2.cloned.1.call-done = bf16[128,6144]{1,0:T(8,128)(2,1)} async-done(((bf16[512,6144]{1,0:T(8,128)(2,1)}), bf16[128,6144]{1,0:T(8,128)(2,1)}) %reduce-scatter.2.cloned.1.call-update) | async-done | bytes 1572880 | tf_op jit(solution)/shard_map/reduce_scatter | solution.py:39
  273.1 3.8 reshape.45
  276.9 91.6 %all_to_all.24 = bf16[32,4,6144]{2,1,0:T(4,128)(2,1)} all-to-all(bf16[32,4,6144]{2,1,0:T(4,128)(2,1)} %reshape.45), channel_id=1, replica_groups=mesh['groups'=2,'expert'=32,'tensor'=4] {'expert'}, dimensions={0} | all-to-all | bytes 3145728 | tf_op jit(solution)/shard_map/all_to_all | solution.py:41
  368.5 3.7 reshape.46
  372.1 2.5 fusion.19
  (9 shorter events, 0.1 us)
Async XLA Ops:
  6.5 200.7 %copy-start = (bf16[1,256,6144]{2,1,0:T(8,128)(2,1)S(1)}, bf16[1,256,6144]{2,1,0:T(8,128)(2,1)}, u32[]{:S(2)}) copy-start(bf16[1,256,6144]{2,1,0:T(8,128)(2,1)} %param.13) | copy-start | bytes 9437188
  6.6 266.5 %reduce-scatter.2.cloned.1.call-start = ((), (), s32[]{:S(2)}) async-start(), calls=%async_computation.4 | async-start | bytes 7864320 | tf_op jit(solution)/shard_map/reduce_scatter | solution.py:39
  128.9 74.7 %copy-start.1 = (bf16[1,6144,256]{2,1,0:T(8,128)(2,1)S(1)}, bf16[1,6144,256]{2,1,0:T(8,128)(2,1)}, u32[]{:S(2)}) copy-start(bf16[1,6144,256]{2,1,0:T(8,128)(2,1)} %param.11) | copy-start | bytes 9437188
  203.5 1.9 copy-start.2
Sparse Core Ops, SparseCore 0:
  211.9 61.1 reduce-scatter.1
